TPU v7x, 256 devices: a 8x8x2 block of a 8x8x16 slice. The times are simulated.
256 devices in a mesh: member: 2 (over z), graph: 64 (over y, x), chan: 2 (over core).
Axes of the slice: x: 8, y: 8, z: 2, core: 2. Of those that a mesh axis runs over, the one named last changes fastest.
The devices are a block of a 8x8x16 slice.
Arguments:
- grid_state: bfloat16 [131072, 256], P(('member', 'graph')), parts along dimension 0, may hold values from -6 to 6
- w_src: bfloat16 [256, 512], P(None, 'chan'), may hold values from -0.375 to 0.375
- bias_src: float32 [512], P('chan'), may hold values from -3 to 3
- mesh_embed: bfloat16 [40960, 512], P('graph', 'chan'), may hold values from -6 to 6
- w_node: bfloat16 [512, 512], P('chan'), may hold values from -0.25 to 0.25
- w_dec: bfloat16 [512, 256], P('chan'), may hold values from -0.125 to 0.125
- slot_src: int32 [64, 64, 128], P('graph'), may hold values from 0 to 1023, as said below
- slot_dst: int32 [64, 64, 128], P(None, 'graph'), may hold values from 0 to 639, as said below
- slot_count: int32 [64, 64], replicated, may hold values from 1 to 128, as said below
Outputs:
- grid_out: bfloat16 [131072, 256], P(('member', 'graph'), 'chan'), parts along dimension 0
There are 2 independent parts, one for each index of `member`. A program takes and returns all parts, laid end to end along the dimension named above; an argument that names none is the same for every part. Nothing has to cross between parts.
Inputs may be any that keep to these rules, and one draw needn't show every extreme that they name: `slot_src`: slots at or past the live count hold arbitrary values in the same range. `slot_dst`: slots at or past the live count hold arbitrary values in the same range. slot_count[s, d] counts the live leading slots of the 128 from shard s to shard d; in every draw some receiving shard has all 128 slots live from every sender.
All inputs are finite; a program needn't handle non-finite values.
Results may differ from a plain program's by a relative error of at most 0.0056.
Values may be sent and summed in bfloat16 or wider, within the bound.
A program may use at most 64 MiB of HBM per device.

v0:
```python
import math
import jax
import jax.numpy as jnp
from jax import lax
from jax.sharding import PartitionSpec as P


def split_up(value, dim, count):
    lengths = value.shape
    parts = value.reshape(*lengths[:dim], count, lengths[dim] // count, *lengths[dim + 1 :])
    return jnp.moveaxis(parts, dim, 0)


def sum_at_owner(value, axis, dim):
    parts = split_up(value, dim, lax.axis_size(axis))
    arrived = lax.all_to_all(parts, axis, split_axis=0, concat_axis=0, tiled=True)
    return arrived.sum(axis=0)


def edge_network(source_rows, w_src, bias_src):
    return jax.nn.silu(
        jnp.dot(source_rows, w_src, preferred_element_type=jnp.float32) + bias_src
    ).astype(jnp.bfloat16)


def segment_rows(values, indices, usable, row_count):
    slot_total = values.shape[0]
    width = values.shape[1]
    block_len = math.gcd(slot_total, 2048)
    block_count = slot_total // block_len
    targets = jnp.where(usable, indices, -1).reshape(block_count, block_len)
    pieces = values.reshape(block_count, block_len, width)
    row_ids = jnp.arange(row_count, dtype=jnp.int32)

    def add_block(summed, scan_item):
        row_target, piece_vals = scan_item
        one_hot = (row_ids[:, None] == row_target[None, :]).astype(jnp.bfloat16)
        return (summed + jnp.dot(one_hot, piece_vals, preferred_element_type=jnp.float32), None)

    result, unused = lax.scan(
        add_block, jnp.zeros((row_count, width), jnp.float32), (targets, pieces)
    )
    return result


def on_device(
    grid_state, w_src, bias_src, mesh_embed, w_node, w_dec, slot_src, slot_dst, slot_count
):
    peers = lax.axis_size("graph")
    own_index = lax.axis_index("graph")
    core_index = lax.axis_index("chan")
    capacity = slot_src.shape[2]
    positions = jnp.arange(capacity, dtype=jnp.int32)
    grid_rows = grid_state.shape[0]
    mesh_rows = mesh_embed.shape[0]
    sent_counts = lax.dynamic_slice_in_dim(slot_count, own_index, 1, 0)[0]
    recv_counts = lax.dynamic_slice_in_dim(slot_count, own_index, 1, 1)[:, 0]
    half_slots = capacity // 2
    chosen = lax.dynamic_slice_in_dim(slot_src[0], core_index * half_slots, half_slots, 1)
    picked = jnp.take(grid_state, chosen.reshape(-1), axis=0).reshape(
        peers, half_slots, grid_state.shape[1]
    )
    arrived = lax.all_to_all(picked, "graph", split_axis=0, concat_axis=0, tiled=True)
    joined = lax.all_gather(arrived, "chan", axis=1, tiled=True)
    messages = edge_network(joined.reshape(peers * capacity, grid_state.shape[1]), w_src, bias_src)
    arrive_ok = (positions[None, :] < recv_counts[:, None]).reshape(-1)
    dst_rows = slot_dst[:, 0, :].reshape(-1)
    aggregate = segment_rows(messages, dst_rows, arrive_ok, mesh_rows)
    partial_hidden = jnp.dot(
        aggregate.astype(jnp.bfloat16), w_node, preferred_element_type=jnp.float32
    )
    hidden_pre = sum_at_owner(partial_hidden, "chan", 1)
    latent = (mesh_embed.astype(jnp.float32) + jax.nn.silu(hidden_pre)).astype(jnp.bfloat16)
    partial_proj = jnp.dot(latent, w_dec, preferred_element_type=jnp.float32)
    projected = sum_at_owner(partial_proj, "chan", 1).astype(jnp.bfloat16)
    returned = jnp.take(projected, dst_rows, axis=0).reshape(peers, capacity, projected.shape[1])
    came_back = lax.all_to_all(returned, "graph", split_axis=0, concat_axis=0, tiled=True).reshape(
        peers * capacity, projected.shape[1]
    )
    send_ok = (positions[None, :] < sent_counts[:, None]).reshape(-1)
    decoded = segment_rows(came_back, slot_src[0].reshape(-1), send_ok, grid_rows)
    width_half = decoded.shape[1]
    own_cols = lax.dynamic_slice_in_dim(grid_state, core_index * width_half, width_half, 1)
    return (own_cols.astype(jnp.float32) + decoded).astype(jnp.bfloat16)


def solution(mesh):
    placed = (
        P(("member", "graph"), None),
        P(None, "chan"),
        P("chan"),
        P("graph", "chan"),
        P("chan", None),
        P("chan", None),
        P("graph", None, None),
        P(None, "graph", None),
        P(),
    )
    return jax.shard_map(
        on_device,
        mesh=mesh,
        in_specs=placed,
        out_specs=P(("member", "graph"), "chan"),
        check_vma=False,
    )
```

profile of v0, /device:TPU:514, one launch (start us, length us, event | category | flops | bytes accessed | tf_op | source)
XLA Modules:
  0.0 256.0 jit_solution(5669027712290382553)
XLA Ops:
  6.6 0.9 compare_and_fusion
  7.6 14.1 %gather_fusion = bf16[4096,256]{1,0:T(8,128)(2,1)S(1)} fusion(bf16[1024,256]{1,0:T(8,128)(2,1)} %param.13, s32[4096]{0:T(1024)S(1)} %broadcast_clamp_fusion.1), kind=kCustom, calls=%fused_computation | custom fusion | bytes 4210688 | tf_op jit(solution)/shard_map/jit(_take)/gather | solution.py:60
  21.7 0.8 broadcast_select_fusion
  22.5 72.0 %all_to_all.20 = bf16[64,64,256]{2,1,0:T(8,128)(2,1)} all-to-all(bf16[64,64,256]{2,1,0:T(8,128)(2,1)S(1)} %broadcast_select_fusion), channel_id=1, replica_groups=mesh['member'=2,'graph'=64,'chan'=2] {'graph'}, dimensions={0} | all-to-all | bytes 4194304 | tf_op jit(solution)/shard_map/all_to_all | solution.py:63
  96.2 0.7 reduce.9
  97.4 25.7 %all-gather.2.cloned.1.call-done = bf16[64,128,256]{2,1,0:T(8,128)(2,1)} async-done(((bf16[64,64,256]{2,1,0:T(8,128)(2,1)}), bf16[64,128,256]{2,1,0:T(8,128)(2,1)}) %all-gather.2.cloned.1.call-update) | async-done | bytes 4194320 | tf_op jit(solution)/shard_map/all_gather | solution.py:64
  123.0 6.1 %multiply_convert_fusion = bf16[8192,256]{1,0:T(8,128)(2,1)} fusion(bf16[8192,256]{1,0:T(8,128)(2,1)} %bitcast.64, bf16[256,256]{1,0:T(8,128)(2,1)S(1)} %copy-done.6, f32[256]{0:T(256)S(1)} %copy-done.8), kind=kOutput, calls=%fused_computation.21 | convolution fusion | flops 1086324736 | bytes 8520704 | tf_op jit(solution)/shard_map/dot_general | solution.py:22
  129.1 9.2 %while.22 = (s32[]{:T(128)}, f32[640,256]{1,0:T(8,128)S(1)}, s32[4,2048]{1,0:T(4,128)S(1)}, bf16[4,2048,256]{2,1,0:T(8,128)(2,1)}, s32[]{:T(128)}, /*index=5*/s32[]{:T(128)}) while((s32[]{:T(128)}, f32[640,256]{1,0:T(8,128)S(1)}, s32[4,2048]{1,0:T(4,128)S(1)}, bf16[4,2048,256]{2,1,0:T(8,128)(2,1)}, s32[]{:T(128)}, ...), condition=%wide.region_1.2_spmd.clone, body=%wide.region_0.1_spmd.clone.sunk | while | flops 672727040 | bytes 2384467 | solution.py:40
  129.1 2.3 fusion.32
  131.4 2.3 fusion.32
  133.8 2.3 fusion.32
  136.1 2.3 fusion.32
  138.8 4.9 %all_to_all.21 = f32[2,640,256]{1,2,0:T(8,128)S(1)} all-to-all(f32[2,640,256]{1,2,0:T(8,128)S(1)} %bitcast.56), channel_id=1, replica_groups=mesh['member'=2,'graph'=64,'chan'=2] {'chan'}, dimensions={0} | all-to-all | bytes 2621440 | tf_op jit(solution)/shard_map/all_to_all | solution.py:16
  144.3 4.3 %all_to_all.22 = f32[2,640,128]{1,2,0:T(8,128)S(1)} all-to-all(f32[2,640,128]{1,2,0:T(8,128)S(1)} %bitcast.58), channel_id=1, replica_groups=mesh['member'=2,'graph'=64,'chan'=2] {'chan'}, dimensions={0} | all-to-all | bytes 1310720 | tf_op jit(solution)/shard_map/all_to_all | solution.py:16
  148.8 24.0 %gather_fusion.1 = bf16[8192,128]{1,0:T(8,128)(2,1)S(1)} fusion(bf16[640,128]{1,0:T(8,128)(2,1)S(1)} %copy.11, s32[8192]{0:T(1024)S(1)} %broadcast_clamp_fusion), kind=kCustom, calls=%fused_computation.1 | custom fusion | bytes 4227072 | tf_op jit(solution)/shard_map/jit(_take)/gather | solution.py:76
  172.8 2.6 %broadcast_select_fusion.1 = bf16[64,128,128]{2,1,0:T(8,128)(2,1)} fusion(bf16[64,128,128]{2,1,0:T(8,128)(2,1)S(1)} %bitcast.54, pred[64,128]{1,0:T(8,128)(4,1)S(1)} %compare_and_fusion.1), kind=kLoop, calls=%fused_computation.23 | loop fusion | flops 1048576 | bytes 4202496 | tf_op jit(solution)/shard_map/jit(_take)/select_n | solution.py:76
  175.5 13.7 %all-to-all-start.3 = ((bf16[64,128,128]{2,1,0:T(8,128)(2,1)}), bf16[64,128,128]{2,1,0:T(8,128)(2,1)S(1)}, u32[]{:S(2)}, u32[]{:S(2)}) async-start(bf16[64,128,128]{2,1,0:T(8,128)(2,1)} %broadcast_select_fusion.1), calls=%async_computation.3 | async-start | bytes 4194304 | tf_op jit(solution)/shard_map/all_to_all | solution.py:77
  189.2 52.1 %all-to-all-done.3 = bf16[64,128,128]{2,1,0:T(8,128)(2,1)S(1)} async-done(((bf16[64,128,128]{2,1,0:T(8,128)(2,1)}), bf16[64,128,128]{2,1,0:T(8,128)(2,1)S(1)}, u32[]{:S(2)}, u32[]{:S(2)}) %all-to-all-start.3) | async-done | bytes 2097184 | tf_op jit(solution)/shard_map/all_to_all | solution.py:77
  241.3 7.0 %while.23 = (s32[]{:T(128)}, f32[1024,128]{1,0:T(8,128)S(1)}, s32[4,2048]{1,0:T(4,128)S(1)}, bf16[4,2048,128]{2,1,0:T(8,128)(2,1)S(1)}, s32[]{:T(128)}, /*index=5*/s32[]{:T(128)}) while((s32[]{:T(128)}, f32[1024,128]{1,0:T(8,128)S(1)}, s32[4,2048]{1,0:T(4,128)S(1)}, bf16[4,2048,128]{2,1,0:T(8,128)(2,1)S(1)}, s32[]{:T(128)}, ...), condition=%wide.region_5.6_spmd.clone, body=%wide.region_4.5_spmd.clone.sunk | while | flops 539230208 | bytes 1597527 | solution.py:40
  241.3 1.7 fusion.34
  243.1 1.7 fusion.34
  244.9 1.7 fusion.34
  246.6 1.7 fusion.34
  248.4 0.8 add_convert_fusion.1
  (52 shorter events, 3.4 us)
Async XLA Ops:
  6.5 131.8 %copy-start = (bf16[256,512]{1,0:T(8,128)(2,1)S(1)}, bf16[256,512]{1,0:T(8,128)(2,1)}, u32[]{:S(2)}) copy-start(bf16[256,512]{1,0:T(8,128)(2,1)} %param.17) | copy-start | bytes 786436
  6.6 116.5 %all-gather.2.cloned.1.call-start = ((), (), s32[]{:S(2)}) async-start(), calls=%async_computation.4 | async-start | bytes 6291456 | tf_op jit(solution)/shard_map/all_gather | solution.py:64
  94.5 0.8 copy-start.4
  94.5 0.8 copy-start.5
  94.5 1.7 copy-start.3
  94.5 2.4 copy-start.2
  94.5 28.5 %copy-start.6 = (bf16[256,256]{1,0:T(8,128)(2,1)S(1)}, bf16[256,256]{1,0:T(8,128)(2,1)}, u32[]{:S(2)}) copy-start(bf16[256,256]{1,0:T(8,128)(2,1)} %param.14) | copy-start | bytes 393220
  94.5 28.5 %copy-start.8 = (f32[256]{0:T(256)S(1)}, f32[256]{0:T(256)}, u32[]{:S(2)}) copy-start(f32[256]{0:T(256)} %param.15) | copy-start | bytes 3076
  138.8 5.1 %copy-start.7 = (bf16[256,256]{1,0:T(8,128)(2,1)S(1)}, bf16[256,256]{1,0:T(8,128)(2,1)}, u32[]{:S(2)}) copy-start(bf16[256,256]{1,0:T(8,128)(2,1)} %param.18) | copy-start | bytes 393220
  175.5 65.9 %all-to-all-start.3 = ((bf16[64,128,128]{2,1,0:T(8,128)(2,1)}), bf16[64,128,128]{2,1,0:T(8,128)(2,1)S(1)}, u32[]{:S(2)}, u32[]{:S(2)}) async-start(bf16[64,128,128]{2,1,0:T(8,128)(2,1)} %broadcast_select_fusion.1), calls=%async_computation.3 | async-start | bytes 4194304 | tf_op jit(solution)/shard_map/all_to_all | solution.py:77
  241.3 7.0 %copy-start.1 = (bf16[1024,256]{1,0:T(8,128)(2,1)S(1)}, bf16[1024,256]{1,0:T(8,128)(2,1)}, u32[]{:S(2)}) copy-start(bf16[1024,256]{1,0:T(8,128)(2,1)} %param.13) | copy-start | bytes 1572868
Sparse Core Ops, SparseCore 0:
  94.7 28.2 all-gather.1
where the time goes:
time: 257 us; the launch traced here: 256 us
  blocking collectives  81.2 us (32%)
  waiting for transfers between devices  77.9 us (30%)
  local copies, waits for them, and re-layouts  40.4 us (16%)
  matrix products  22.8 us (9%)
  starting transfers between devices  13.7 us (5%)
  between operations  13.7 us (5%)
  other arithmetic  6.13 us (2%)
    all_to_all x1, blocking collectives, on_device(): lax.all_to_all(picked, 'graph', split_axis=0, concat_axis=0, tiled=True)  72 us
    all_to_all x1, waiting for transfers between devices, on_device(): lax.all_to_all(returned, 'graph', split_axis=0, concat_axis=0, tiled=True)  52.1 us
    all_gather x1, waiting for transfers between devices, on_device(): joined = lax.all_gather(arrived, 'chan', axis=1, tiled=True)  25.7 us
    gather x1, local copies, waits for them, and re-layouts, on_device(): jnp.take(projected, dst_rows, axis=0)  24 us
    dot_general x8, matrix products, add_block(): jnp.dot(one_hot, piece_vals, preferred_element_type=jnp.float32)  15.9 us
    gather x1, local copies, waits for them, and re-layouts, on_device(): jnp.take(grid_state, chosen.reshape(-1), axis=0)  14.1 us
    all_to_all x1, starting transfers between devices, on_device(): lax.all_to_all(returned, 'graph', split_axis=0, concat_axis=0, tiled=True)  13.7 us
    all_to_all x2, blocking collectives, sum_at_owner(): lax.all_to_all(parts, axis, split_axis=0, concat_axis=0, tiled=True)  9.21 us
  transfers between devices with their start and end apart: 2, of which 2 were waited for; matrix products, arithmetic and copies ran while one was open for 1% of the time, Pallas kernels for 0%

commit v1 on v0

--- a/solution.py
+++ b/solution.py
@@ -1,8 +1,21 @@
+import functools
 import math
 import jax
 import jax.numpy as jnp
 from jax import lax
 from jax.sharding import PartitionSpec as P
+
+
+def _handle_words(x0, shard_axis, axis_k):
+    extent = lax.axis_size(shard_axis)
+    windows = tuple((extent if i0 == axis_k else 1 for i0 in range(x0.ndim)))
+    piece_next = jnp.tile(x0, windows)
+    return lax.all_to_all(
+        piece_next, axis_name=shard_axis, split_axis=axis_k, concat_axis=axis_k, tiled=True
+    )
+
+
+carry_heads = functools.partial(_handle_words, shard_axis="chan", axis_k=1)
 
 
 def split_up(value, dim, count):
@@ -61,7 +74,7 @@
         peers, half_slots, grid_state.shape[1]
     )
     arrived = lax.all_to_all(picked, "graph", split_axis=0, concat_axis=0, tiled=True)
-    joined = lax.all_gather(arrived, "chan", axis=1, tiled=True)
+    joined = carry_heads(arrived)
     messages = edge_network(joined.reshape(peers * capacity, grid_state.shape[1]), w_src, bias_src)
     arrive_ok = (positions[None, :] < recv_counts[:, None]).reshape(-1)
     dst_rows = slot_dst[:, 0, :].reshape(-1)

time: 257 us -> 223 us (0.87)
  blocking collectives: 81.2 us -> 16.3 us
  starting transfers between devices: 13.7 us -> 33.8 us
  waiting for transfers between devices: 77.9 us -> 97.2 us
  between operations: 13.7 us -> 0.28 us
  local copies, waits for them, and re-layouts: 40.4 us -> 44.6 us
    all_to_all x1, blocking collectives: 72 us -> 7.12 us  [_handle_words(): lax.all_to_all(piece_next, axis_name=shard_axis, split_axis=axis_k, conca...]
    all_to_all x0 -> x1, waiting for transfers between devices: none -> 45 us  [on_device(): lax.all_to_all(picked, 'graph', split_axis=0, concat_axis=0, tiled=True)]
    all_gather x1 -> x0, waiting for transfers between devices: 25.7 us -> none  [on_device(): joined = lax.all_gather(arrived, 'chan', axis=1, tiled=True)]
    all_to_all x0 -> x1, starting transfers between devices: none -> 24.4 us  [on_device(): lax.all_to_all(picked, 'graph', split_axis=0, concat_axis=0, tiled=True)]
    all_to_all x1, starting transfers between devices: 13.7 us -> 9.35 us  [on_device(): lax.all_to_all(returned, 'graph', split_axis=0, concat_axis=0, tiled=True)]
    all_to_all x0 -> x2, local copies, waits for them, and re-layouts: none -> 3.62 us  [the longest x1 2.44 us: _handle_words(): lax.all_to_all(piece_next, axis_name=shard_axis, split_axis=axis_k, conca...]
where the time goes in v1:
time: 223 us; the launch traced here: 220 us
  waiting for transfers between devices  97.2 us (44%)
  local copies, waits for them, and re-layouts  44.6 us (20%)
  starting transfers between devices  33.8 us (15%)
  matrix products  20.7 us (9%)
  blocking collectives  16.3 us (7%)
  other arithmetic  7.02 us (3%)
    all_to_all x1, waiting for transfers between devices, on_device(): lax.all_to_all(returned, 'graph', split_axis=0, concat_axis=0, tiled=True)  52.1 us
    all_to_all x1, waiting for transfers between devices, on_device(): lax.all_to_all(picked, 'graph', split_axis=0, concat_axis=0, tiled=True)  45 us
    all_to_all x1, starting transfers between devices, on_device(): lax.all_to_all(picked, 'graph', split_axis=0, concat_axis=0, tiled=True)  24.4 us
    gather x1, local copies, waits for them, and re-layouts, on_device(): jnp.take(projected, dst_rows, axis=0)  24 us
    dot_general x8, matrix products, add_block(): jnp.dot(one_hot, piece_vals, preferred_element_type=jnp.float32)  15.9 us
    gather x1, local copies, waits for them, and re-layouts, on_device(): jnp.take(grid_state, chosen.reshape(-1), axis=0)  14.1 us
    all_to_all x1, starting transfers between devices, on_device(): lax.all_to_all(returned, 'graph', split_axis=0, concat_axis=0, tiled=True)  9.35 us
    all_to_all x2, blocking collectives, sum_at_owner(): lax.all_to_all(parts, axis, split_axis=0, concat_axis=0, tiled=True)  9.21 us
  transfers between devices with their start and end apart: 2, of which 2 were waited for; matrix products, arithmetic and copies ran while one was open for 1% of the time, Pallas kernels for 0%

profile of v1, /device:TPU:514, one launch (start us, length us, event | category | flops | bytes accessed | tf_op | source)
XLA Modules:
  0.0 220.1 jit_solution(252606315963969498)
XLA Ops:
  1.0 14.1 %gather_fusion = bf16[4096,256]{1,0:T(8,128)(2,1)S(1)} fusion(bf16[1024,256]{1,0:T(8,128)(2,1)} %param.13, s32[4096]{0:T(1024)S(1)} %broadcast_clamp_fusion.1), kind=kCustom, calls=%fused_computation | custom fusion | bytes 4210688 | tf_op jit(solution)/shard_map/jit(_take)/gather | solution.py:73
  15.1 1.7 broadcast_select_fusion
  16.9 24.4 %all-to-all-start = ((bf16[64,64,256]{2,1,0:T(8,128)(2,1)}), bf16[64,64,256]{2,1,0:T(8,128)(2,1)S(1)}, u32[]{:S(2)}, u32[]{:S(2)}) async-start(bf16[64,64,256]{2,1,0:T(8,128)(2,1)} %broadcast_select_fusion), calls=%async_computation | async-start | bytes 4194304 | tf_op jit(solution)/shard_map/all_to_all | solution.py:76
  44.1 45.0 %all-to-all-done = bf16[64,64,256]{2,1,0:T(8,128)(2,1)S(1)} async-done(((bf16[64,64,256]{2,1,0:T(8,128)(2,1)}), bf16[64,64,256]{2,1,0:T(8,128)(2,1)S(1)}, u32[]{:S(2)}, u32[]{:S(2)}) %all-to-all-start) | async-done | bytes 2097184 | tf_op jit(solution)/shard_map/all_to_all | solution.py:76
  89.2 1.2 copy.14
  90.9 7.1 %all_to_all.25 = bf16[64,128,256]{2,0,1:T(8,128)(2,1)S(1)} all-to-all(bf16[64,128,256]{2,0,1:T(8,128)(2,1)S(1)} %bitcast.55), channel_id=1, replica_groups=mesh['member'=2,'graph'=64,'chan'=2] {'chan'}, dimensions={1} | all-to-all | bytes 8388608 | tf_op jit(solution)/shard_map/all_to_all | solution.py:13
  98.0 2.4 %copy.15 = bf16[64,128,256]{2,1,0:T(8,128)(2,1)S(1)} copy(bf16[64,128,256]{2,0,1:T(8,128)(2,1)S(1)} %all_to_all.25) | data formatting | bytes 8388608 | tf_op jit(solution)/shard_map/all_to_all | solution.py:13
  100.5 4.0 %multiply_convert_fusion = bf16[8192,256]{1,0:T(8,128)(2,1)} fusion(bf16[8192,256]{1,0:T(8,128)(2,1)S(1)} %bitcast.59, bf16[256,256]{1,0:T(8,128)(2,1)S(1)} %copy-done.7, f32[256]{0:T(256)S(1)} %copy-done.9), kind=kOutput, calls=%fused_computation.21 | convolution fusion | flops 1086324736 | bytes 8520704 | tf_op jit(solution)/shard_map/dot_general | solution.py:35
  104.4 9.2 %while.22 = (s32[]{:T(128)}, f32[640,256]{1,0:T(8,128)S(1)}, s32[4,2048]{1,0:T(4,128)S(1)}, bf16[4,2048,256]{2,1,0:T(8,128)(2,1)}, s32[]{:T(128)}, /*index=5*/s32[]{:T(128)}) while((s32[]{:T(128)}, f32[640,256]{1,0:T(8,128)S(1)}, s32[4,2048]{1,0:T(4,128)S(1)}, bf16[4,2048,256]{2,1,0:T(8,128)(2,1)}, s32[]{:T(128)}, ...), condition=%wide.region_1.2_spmd.clone, body=%wide.region_0.1_spmd.clone.sunk | while | flops 672727040 | bytes 2384467 | solution.py:53
  104.4 2.3 %fusion.32 = f32[640,256]{1,0:T(8,128)S(1)} fusion(s32[2048]{0:T(1024)S(1)} %bitcast.63, bf16[4,2048,256]{2,1,0:T(8,128)(2,1)} %get-tuple-element.182, s32[]{:T(128)} %get-tuple-element.173, f32[640,256]{1,0:T(8,128)S(1)} %get-tuple-element.174, pred[]{:T(512)S(6)} %compare.6), kind=kOutput, calls=%fused_computation.7.clone.1 | convolution fusion | flops 672727040 | bytes 2368001 | tf_op jit(solution)/shard_map/while/body/eval_jaxpr/dot_general | solution.py:51
  106.8 2.3 %fusion.32 = f32[640,256]{1,0:T(8,128)S(1)} fusion(s32[2048]{0:T(1024)S(1)} %bitcast.63, bf16[4,2048,256]{2,1,0:T(8,128)(2,1)} %get-tuple-element.182, s32[]{:T(128)} %get-tuple-element.173, f32[640,256]{1,0:T(8,128)S(1)} %get-tuple-element.174, pred[]{:T(512)S(6)} %compare.6), kind=kOutput, calls=%fused_computation.7.clone.1 | convolution fusion | flops 672727040 | bytes 2368001 | tf_op jit(solution)/shard_map/while/body/eval_jaxpr/dot_general | solution.py:51
  109.1 2.3 %fusion.32 = f32[640,256]{1,0:T(8,128)S(1)} fusion(s32[2048]{0:T(1024)S(1)} %bitcast.63, bf16[4,2048,256]{2,1,0:T(8,128)(2,1)} %get-tuple-element.182, s32[]{:T(128)} %get-tuple-element.173, f32[640,256]{1,0:T(8,128)S(1)} %get-tuple-element.174, pred[]{:T(512)S(6)} %compare.6), kind=kOutput, calls=%fused_computation.7.clone.1 | convolution fusion | flops 672727040 | bytes 2368001 | tf_op jit(solution)/shard_map/while/body/eval_jaxpr/dot_general | solution.py:51
  111.4 2.3 %fusion.32 = f32[640,256]{1,0:T(8,128)S(1)} fusion(s32[2048]{0:T(1024)S(1)} %bitcast.63, bf16[4,2048,256]{2,1,0:T(8,128)(2,1)} %get-tuple-element.182, s32[]{:T(128)} %get-tuple-element.173, f32[640,256]{1,0:T(8,128)S(1)} %get-tuple-element.174, pred[]{:T(512)S(6)} %compare.6), kind=kOutput, calls=%fused_computation.7.clone.1 | convolution fusion | flops 672727040 | bytes 2368001 | tf_op jit(solution)/shard_map/while/body/eval_jaxpr/dot_general | solution.py:51
  114.1 4.9 %all_to_all.26 = f32[2,640,256]{1,2,0:T(8,128)S(1)} all-to-all(f32[2,640,256]{1,2,0:T(8,128)S(1)} %bitcast.58), channel_id=1, replica_groups=mesh['member'=2,'graph'=64,'chan'=2] {'chan'}, dimensions={0} | all-to-all | bytes 2621440 | tf_op jit(solution)/shard_map/all_to_all | solution.py:29
  119.6 4.3 %all_to_all.27 = f32[2,640,128]{1,2,0:T(8,128)S(1)} all-to-all(f32[2,640,128]{1,2,0:T(8,128)S(1)} %bitcast.61), channel_id=1, replica_groups=mesh['member'=2,'graph'=64,'chan'=2] {'chan'}, dimensions={0} | all-to-all | bytes 1310720 | tf_op jit(solution)/shard_map/all_to_all | solution.py:29
  124.1 24.0 %gather_fusion.1 = bf16[8192,128]{1,0:T(8,128)(2,1)S(1)} fusion(bf16[640,128]{1,0:T(8,128)(2,1)S(1)} %copy.16, s32[8192]{0:T(1024)S(1)} %broadcast_clamp_fusion), kind=kCustom, calls=%fused_computation.1 | custom fusion | bytes 4227072 | tf_op jit(solution)/shard_map/jit(_take)/gather | solution.py:89
  148.2 2.6 %broadcast_select_fusion.1 = bf16[64,128,128]{2,1,0:T(8,128)(2,1)} fusion(bf16[64,128,128]{2,1,0:T(8,128)(2,1)S(1)} %bitcast.56, pred[64,128]{1,0:T(8,128)(4,1)S(1)} %compare_and_fusion.1), kind=kLoop, calls=%fused_computation.23 | loop fusion | flops 1048576 | bytes 4202496 | tf_op jit(solution)/shard_map/jit(_take)/select_n | solution.py:89
  150.8 9.3 %all-to-all-start.4 = ((bf16[64,128,128]{2,1,0:T(8,128)(2,1)}), bf16[64,128,128]{2,1,0:T(8,128)(2,1)S(1)}, u32[]{:S(2)}, u32[]{:S(2)}) async-start(bf16[64,128,128]{2,1,0:T(8,128)(2,1)} %broadcast_select_fusion.1), calls=%async_computation.4 | async-start | bytes 4194304 | tf_op jit(solution)/shard_map/all_to_all | solution.py:90
  160.2 52.1 %all-to-all-done.4 = bf16[64,128,128]{2,1,0:T(8,128)(2,1)S(1)} async-done(((bf16[64,128,128]{2,1,0:T(8,128)(2,1)}), bf16[64,128,128]{2,1,0:T(8,128)(2,1)S(1)}, u32[]{:S(2)}, u32[]{:S(2)}) %all-to-all-start.4) | async-done | bytes 2097184 | tf_op jit(solution)/shard_map/all_to_all | solution.py:90
  212.3 7.0 %while.23 = (s32[]{:T(128)}, f32[1024,128]{1,0:T(8,128)S(1)}, s32[4,2048]{1,0:T(4,128)S(1)}, bf16[4,2048,128]{2,1,0:T(8,128)(2,1)S(1)}, s32[]{:T(128)}, /*index=5*/s32[]{:T(128)}) while((s32[]{:T(128)}, f32[1024,128]{1,0:T(8,128)S(1)}, s32[4,2048]{1,0:T(4,128)S(1)}, bf16[4,2048,128]{2,1,0:T(8,128)(2,1)S(1)}, s32[]{:T(128)}, ...), condition=%wide.region_5.6_spmd.clone, body=%wide.region_4.5_spmd.clone.sunk | while | flops 539230208 | bytes 1597527 | solution.py:53
  212.3 1.7 fusion.34
  214.1 1.7 fusion.34
  215.9 1.7 fusion.34
  217.6 1.7 fusion.34
  (56 shorter events, 6.3 us)
Async XLA Ops:
  0.0 113.7 %copy-start = (bf16[256,512]{1,0:T(8,128)(2,1)S(1)}, bf16[256,512]{1,0:T(8,128)(2,1)}, u32[]{:S(2)}) copy-start(bf16[256,512]{1,0:T(8,128)(2,1)} %param.17) | copy-start | bytes 786436
  16.9 24.5 %copy-start.5 = (s32[1,64,128]{2,1,0:T(8,128)S(1)}, s32[1,64,128]{2,1,0:T(8,128)}, u32[]{:S(2)}) copy-start(s32[1,64,128]{2,1,0:T(8,128)} %param.19) | copy-start | bytes 98308
  16.9 24.5 %copy-start.6 = (s32[64,64]{1,0:T(8,128)S(1)}, s32[64,64]{1,0:T(8,128)}, u32[]{:S(2)}) copy-start(s32[64,64]{1,0:T(8,128)} %param.21) | copy-start | bytes 49156
  16.9 25.4 %copy-start.4 = (s32[64,1,128]{2,1,0:T(1,128)S(1)}, s32[64,1,128]{2,1,0:T(1,128)}, u32[]{:S(2)}) copy-start(s32[64,1,128]{2,1,0:T(1,128)} %param.20) | copy-start | bytes 98308
  16.9 26.1 %copy-start.2 = (bf16[640,256]{1,0:T(8,128)(2,1)S(1)}, bf16[640,256]{1,0:T(8,128)(2,1)}, u32[]{:S(2)}) copy-start(bf16[640,256]{1,0:T(8,128)(2,1)} %param.16) | copy-start | bytes 983044
  16.9 72.3 %all-to-all-start = ((bf16[64,64,256]{2,1,0:T(8,128)(2,1)}), bf16[64,64,256]{2,1,0:T(8,128)(2,1)S(1)}, u32[]{:S(2)}, u32[]{:S(2)}) async-start(bf16[64,64,256]{2,1,0:T(8,128)(2,1)} %broadcast_select_fusion), calls=%async_computation | async-start | bytes 4194304 | tf_op jit(solution)/shard_map/all_to_all | solution.py:76
  98.0 2.4 %copy-start.7 = (bf16[256,256]{1,0:T(8,128)(2,1)S(1)}, bf16[256,256]{1,0:T(8,128)(2,1)}, u32[]{:S(2)}) copy-start(bf16[256,256]{1,0:T(8,128)(2,1)} %param.14) | copy-start | bytes 393220
  98.0 2.5 %copy-start.9 = (f32[256]{0:T(256)S(1)}, f32[256]{0:T(256)}, u32[]{:S(2)}) copy-start(f32[256]{0:T(256)} %param.15) | copy-start | bytes 3076
  114.1 5.1 %copy-start.3 = (bf16[640,256]{0,1:T(8,128)(2,1)S(1)}, bf16[640,256]{0,1:T(8,128)(2,1)}, u32[]{:S(2)}) copy-start(bf16[640,256]{0,1:T(8,128)(2,1)} %copy.13) | copy-start | bytes 983044
  114.1 5.1 %copy-start.8 = (bf16[256,256]{1,0:T(8,128)(2,1)S(1)}, bf16[256,256]{1,0:T(8,128)(2,1)}, u32[]{:S(2)}) copy-start(bf16[256,256]{1,0:T(8,128)(2,1)} %param.18) | copy-start | bytes 393220
  150.8 61.5 %all-to-all-start.4 = ((bf16[64,128,128]{2,1,0:T(8,128)(2,1)}), bf16[64,128,128]{2,1,0:T(8,128)(2,1)S(1)}, u32[]{:S(2)}, u32[]{:S(2)}) async-start(bf16[64,128,128]{2,1,0:T(8,128)(2,1)} %broadcast_select_fusion.1), calls=%async_computation.4 | async-start | bytes 4194304 | tf_op jit(solution)/shard_map/all_to_all | solution.py:90
  212.3 7.0 %copy-start.1 = (bf16[1024,256]{1,0:T(8,128)(2,1)S(1)}, bf16[1024,256]{1,0:T(8,128)(2,1)}, u32[]{:S(2)}) copy-start(bf16[1024,256]{1,0:T(8,128)(2,1)} %param.13) | copy-start | bytes 1572868
